TPU v7x, 512 devices: a whole 4x8x8 slice. The times are simulated.
512 devices in a mesh: grp: 32 (over z, x_hi, core), mem: 16 (over y, x_lo).
Axes of the slice: x: 4 (x_hi: 2, x_lo: 2; x = x_hi * 2 + x_lo), y: 8, z: 8, core: 2. Of those that a mesh axis runs over, the one named last changes fastest.
Arguments:
- hidden_grads: bfloat16 [65536, 2048], P(('grp', 'mem')), may hold values from -56 to 56
- weight_grad: bfloat16 [2048, 6144], P('mem', 'grp'), may hold values from -6 to 6
Outputs:
- inverse_root: float32 [2048, 2048], P('mem', 'grp')
- conditioned: float32 [2048, 6144], P('mem', 'grp')
All inputs are finite; a program needn't handle non-finite values.
Results may differ from a plain program's by a relative error of at most 0.0003.
Values may be sent and summed in bfloat16 or wider, within the bound.
A program may use at most 64 MiB of HBM per device.

v0:
```python
import functools

import jax
import jax.numpy as jnp
from jax import lax
from jax.sharding import Mesh
from jax.sharding import PartitionSpec as P

GRP = ("grp_0", "grp_1", "grp_2")
MEM = ("mem_0", "mem_1")
GRP_MEM = ("grp_0", "grp_1", "grp_2", "mem_0", "mem_1")


exact_mode = lax.Precision.HIGHEST


def over_axes(x, axes):
    return functools.reduce(lax.psum, axes, x)


def gather_axes(x, axes, dim):
    for axis in reversed(axes):
        x = lax.all_gather(x, axis, axis=dim, tiled=True)
    return x


def in_blocks(x, dim, devices):
    dims = x.shape
    blocks = x.reshape(*dims[:dim], devices, dims[dim] // devices, *dims[dim + 1 :])
    return jnp.moveaxis(blocks, dim, 0)


def summed_on_arrival(x, axis, dim):
    blocks = in_blocks(x, dim, lax.axis_size(axis))
    arrived = lax.all_to_all(blocks, axis, split_axis=0, concat_axis=0, tiled=True)
    return arrived.sum(axis=0)


def sent_to_all(x, axis):
    copies = jnp.broadcast_to(x, (lax.axis_size(axis), *x.shape))
    return lax.all_to_all(copies, axis, split_axis=0, concat_axis=0, tiled=True)


def joined_along(blocks, dim):
    blocks = jnp.moveaxis(blocks, 0, dim)
    dims = blocks.shape
    return blocks.reshape(*dims[:dim], dims[dim] * dims[dim + 1], *dims[dim + 2 :])


def gathered_copies(x, axis, dim):
    blocks = sent_to_all(x, axis)
    return joined_along(blocks, dim)


def product(left_part, right_part):
    return jnp.dot(left_part, right_part, precision=exact_mode)


def on_device(hidden_grads, weight_grad):
    row_count = weight_grad.shape[0]
    block_order = hidden_grads.shape[1]
    col_count = block_order // lax.axis_size(GRP)
    row_start = lax.axis_index(MEM) * row_count
    col_start = lax.axis_index(GRP) * col_count
    widened = hidden_grads.astype(jnp.float32)
    total_sq = over_axes(jnp.sum(widened * widened), GRP_MEM)
    block_rows = gather_axes(hidden_grads, MEM, 0)
    own_cols = lax.dynamic_slice_in_dim(block_rows, row_start, row_count, 1)
    partial_value = lax.dot_general(
        own_cols, block_rows, (((0,), (0,)), ((), ())), preferred_element_type=jnp.float32
    )
    factor_scale = block_order / (6.0 * total_sq)
    cov_tile = summed_on_arrival(partial_value, GRP, 1) * factor_scale
    cov_panel = lax.all_gather(cov_tile, GRP, axis=1, tiled=True)
    row_ids = row_start + lax.iota(jnp.int32, row_count)
    col_ids = col_start + lax.iota(jnp.int32, col_count)
    every_id = lax.iota(jnp.int32, block_order)
    unit_rows = (row_ids[:, None] == every_id[None, :]).astype(jnp.float32)
    unit_tile = (row_ids[:, None] == col_ids[None, :]).astype(jnp.float32)
    unit_cols = (every_id[:, None] == col_ids[None, :]).astype(jnp.float32)
    first_cols = lax.all_gather(cov_tile, MEM, axis=0, tiled=True)
    step_row = 1.5 * unit_rows - 0.5 * cov_panel
    next_tile = product(step_row, first_cols)
    root_cols = 1.5 * unit_cols - 0.5 * first_cols
    next_cols = lax.all_gather(next_tile, MEM, axis=0, tiled=True)
    mixed_tile = 1.5 * unit_tile - 0.5 * product(step_row, next_cols)
    mixed_rows = gathered_copies(mixed_tile, GRP, 1)
    root_tile = product(mixed_rows, root_cols)
    grad_cols = lax.all_gather(weight_grad, MEM, axis=0, tiled=True)
    half_tile = product(step_row, grad_cols.astype(jnp.float32))
    half_cols = gathered_copies(half_tile, MEM, 0)
    result = product(mixed_rows, half_cols)
    return (root_tile, result)


def solution(mesh):
    finer = Mesh(mesh.devices.reshape(8, 2, 2, 8, 2), ("grp_0", "grp_1", "grp_2", "mem_0", "mem_1"))
    placed = (P(GRP_MEM, None), P(MEM, GRP))
    return jax.shard_map(
        on_device,
        mesh=finer,
        in_specs=placed,
        out_specs=(P(MEM, GRP), P(MEM, GRP)),
        check_vma=False,
    )
```

profile of v0, /device:TPU:1, one launch (start us, length us, event | category | flops | bytes accessed | tf_op | source)
XLA Modules:
  0.0 448.6 jit_solution(1549481817835514991)
XLA Ops:
  7.9 36.6 %all-gather.4.cloned.1.call-done = bf16[256,2048]{1,0:T(8,128)(2,1)} async-done(((bf16[128,2048]{1,0:T(8,128)(2,1)}), bf16[256,2048]{1,0:T(8,128)(2,1)}) %all-gather.4.cloned.1.call-update) | async-done | bytes 1048592 | tf_op jit(solution)/shard_map/all_gather | solution.py:23
  44.6 99.5 %all-gather.6.cloned.1.call-done = bf16[2048,2048]{1,0:T(8,128)(2,1)} async-done(((bf16[256,2048]{1,0:T(8,128)(2,1)}), bf16[2048,2048]{1,0:T(8,128)(2,1)}) %all-gather.6.cloned.1.call-update) | async-done | bytes 8388624 | tf_op jit(solution)/shard_map/all_gather | solution.py:23
  144.1 8.0 %fusion.13 = f32[128,2048]{0,1:T(8,128)} fusion(bf16[2048,2048]{1,0:T(8,128)(2,1)} %all-gather.6.cloned.1.call-done, s32[]{:T(128)S(6)} %select_n.3), kind=kOutput, calls=%fused_computation.18 | convolution fusion | flops 1073741824 | bytes 9961476 | tf_op jit(solution)/shard_map/dot_general | solution.py:69
  152.1 10.9 %all-to-all-start = ((f32[32,128,64]{1,2,0:T(8,128)}), f32[32,128,64]{1,2,0:T(8,128)S(1)}, u32[]{:S(2)}, u32[]{:S(2)}) async-start(f32[32,128,64]{1,2,0:T(8,128)} %bitcast.1), calls=%async_computation | async-start | bytes 2097152 | tf_op jit(solution)/shard_map/all_to_all | solution.py:35
  163.1 0.9 multiply_reduce_fusion
  163.9 31.9 %psum.35 = f32[]{:T(128)} all-reduce(f32[]{:T(128)} %multiply_reduce_fusion), channel_id=1, replica_groups=mesh['grp_0'=8,'grp_1'=2,'grp_2'=2,'mem_0'=8,'mem_1'=2] {'grp_0'}, use_global_device_ids=true, to_apply=%region_2.0 | all-reduce | flops 1 | bytes 8 | tf_op jit(solution)/shard_map/psum | solution.py:18
  195.9 6.1 %psum.36 = f32[]{:T(128)} all-reduce(f32[]{:T(128)} %psum.35), channel_id=1, replica_groups=mesh['grp_0'=8,'grp_1'=2,'grp_2'=2,'mem_0'=8,'mem_1'=2] {'grp_1'}, use_global_device_ids=true, to_apply=%region_3.0 | all-reduce | flops 1 | bytes 8 | tf_op jit(solution)/shard_map/psum | solution.py:18
  202.0 7.4 %psum.37 = f32[]{:T(128)} all-reduce(f32[]{:T(128)} %psum.36), channel_id=1, replica_groups=mesh['grp_0'=8,'grp_1'=2,'grp_2'=2,'mem_0'=8,'mem_1'=2] {'grp_2'}, use_global_device_ids=true, to_apply=%region_4.0 | all-reduce | flops 1 | bytes 8 | tf_op jit(solution)/shard_map/psum | solution.py:18
  209.3 12.4 %psum.38 = f32[]{:T(128)} all-reduce(f32[]{:T(128)} %psum.37), channel_id=1, replica_groups=mesh['grp_0'=8,'grp_1'=2,'grp_2'=2,'mem_0'=8,'mem_1'=2] {'mem_0'}, use_global_device_ids=true, to_apply=%region_5.0 | all-reduce | flops 1 | bytes 8 | tf_op jit(solution)/shard_map/psum | solution.py:18
  221.8 4.4 psum.39
  227.6 26.8 %all_gather.21 = f32[2048,64]{0,1:T(8,128)S(1)} all-gather(f32[128,64]{0,1:T(8,128)} %broadcast_multiply_fusion), channel_id=1, replica_groups=mesh['grp_0'=8,'grp_1'=2,'grp_2'=2,'mem_0'=8,'mem_1'=2] {'mem_0','mem_1'}, dimensions={0}, use_global_device_ids=true | all-gather | bytes 557056 | tf_op jit(solution)/shard_map/all_gather | solution.py:81
  254.4 61.1 %all-gather.8.cloned.1.call-done = f32[128,2048]{0,1:T(8,128)} async-done(((f32[128,64]{0,1:T(8,128)}), f32[128,2048]{0,1:T(8,128)}) %all-gather.8.cloned.1.call-update) | async-done | bytes 1048592 | tf_op jit(solution)/shard_map/all_gather | solution.py:74
  315.5 2.2 fusion.5
  317.8 27.9 %all_gather.22 = f32[2048,64]{0,1:T(8,128)S(1)} all-gather(f32[128,64]{0,1:T(8,128)S(1)} %fusion.5), channel_id=1, replica_groups=mesh['grp_0'=8,'grp_1'=2,'grp_2'=2,'mem_0'=8,'mem_1'=2] {'mem_0','mem_1'}, dimensions={0}, use_global_device_ids=true | all-gather | bytes 557056 | tf_op jit(solution)/shard_map/all_gather | solution.py:85
  345.7 0.9 fusion.3
  346.7 1.1 broadcast_in_dim.4
  347.8 13.7 %all-to-all-start.1 = ((f32[32,128,64]{1,2,0:T(8,128)}), f32[32,128,64]{1,2,0:T(8,128)S(1)}, u32[]{:S(2)}, u32[]{:S(2)}) async-start(f32[32,128,64]{1,2,0:T(8,128)} %broadcast_in_dim.4), calls=%async_computation.1 | async-start | bytes 2097152 | tf_op jit(solution)/shard_map/all_to_all | solution.py:41
  361.5 35.8 %all_gather.23 = bf16[2048,192]{0,1:T(8,128)(2,1)S(1)} all-gather(bf16[128,192]{0,1:T(8,128)(2,1)S(1)} %copy-done.2), channel_id=1, replica_groups=mesh['grp_0'=8,'grp_1'=2,'grp_2'=2,'mem_0'=8,'mem_1'=2] {'mem_0','mem_1'}, dimensions={0}, use_global_device_ids=true | all-gather | bytes 835584 | tf_op jit(solution)/shard_map/all_gather | solution.py:89
  397.3 1.0 fusion.4
  398.3 1.3 broadcast_in_dim.5
  399.6 5.7 %all-to-all-start.2 = ((f32[16,128,192]{1,2,0:T(8,128)}), f32[16,128,192]{1,2,0:T(8,128)S(1)}, u32[]{:S(2)}, u32[]{:S(2)}) async-start(f32[16,128,192]{1,2,0:T(8,128)} %broadcast_in_dim.5), calls=%async_computation.2 | async-start | bytes 3145728 | tf_op jit(solution)/shard_map/all_to_all | solution.py:41
  405.3 1.5 fusion.6
  406.8 33.2 %all-to-all-done.2 = f32[16,128,192]{1,2,0:T(8,128)S(1)} async-done(((f32[16,128,192]{1,2,0:T(8,128)}), f32[16,128,192]{1,2,0:T(8,128)S(1)}, u32[]{:S(2)}, u32[]{:S(2)}) %all-to-all-start.2) | async-done | bytes 1572896 | tf_op jit(solution)/shard_map/all_to_all | solution.py:41
  440.0 2.0 fusion
  (18 shorter events, 1.6 us)
Async XLA Ops:
  7.2 37.4 %all-gather.4.cloned.1.call-start = ((), (), s32[]{:S(2)}) async-start(), calls=%async_computation.3 | async-start | bytes 1572864 | tf_op jit(solution)/shard_map/all_gather | solution.py:23
  7.9 136.2 %all-gather.6.cloned.1.call-start = ((), (), s32[]{:S(2)}) async-start(), calls=%async_computation.4 | async-start | bytes 9437184 | tf_op jit(solution)/shard_map/all_gather | solution.py:23
  152.1 11.0 %copy-start.1 = (bf16[128,2048]{1,0:T(8,128)(2,1)S(1)}, bf16[128,2048]{1,0:T(8,128)(2,1)}, u32[]{:S(2)}) copy-start(bf16[128,2048]{1,0:T(8,128)(2,1)} %param.2) | copy-start | bytes 1572868
  152.1 74.8 %all-to-all-start = ((f32[32,128,64]{1,2,0:T(8,128)}), f32[32,128,64]{1,2,0:T(8,128)S(1)}, u32[]{:S(2)}, u32[]{:S(2)}) async-start(f32[32,128,64]{1,2,0:T(8,128)} %bitcast.1), calls=%async_computation | async-start | bytes 2097152 | tf_op jit(solution)/shard_map/all_to_all | solution.py:35
  163.0 152.5 %all-gather.8.cloned.1.call-start = ((), (), s32[]{:S(2)}) async-start(), calls=%async_computation.5 | async-start | bytes 1081344 | tf_op jit(solution)/shard_map/all_gather | solution.py:74
  315.5 30.2 %copy-start = (f32[128,2048]{0,1:T(8,128)S(1)}, f32[128,2048]{0,1:T(8,128)}, u32[]{:S(2)}) copy-start(f32[128,2048]{0,1:T(8,128)} %all-gather.8.cloned.1.call-done) | copy-start | bytes 3145732
  346.7 14.8 %copy-start.2 = (bf16[128,192]{0,1:T(8,128)(2,1)S(1)}, bf16[128,192]{0,1:T(8,128)(2,1)}, u32[]{:S(2)}) copy-start(bf16[128,192]{0,1:T(8,128)(2,1)} %param.3) | copy-start | bytes 147460
  347.8 50.5 %all-to-all-start.1 = ((f32[32,128,64]{1,2,0:T(8,128)}), f32[32,128,64]{1,2,0:T(8,128)S(1)}, u32[]{:S(2)}, u32[]{:S(2)}) async-start(f32[32,128,64]{1,2,0:T(8,128)} %broadcast_in_dim.4), calls=%async_computation.1 | async-start | bytes 2097152 | tf_op jit(solution)/shard_map/all_to_all | solution.py:41
  399.6 40.4 %all-to-all-start.2 = ((f32[16,128,192]{1,2,0:T(8,128)}), f32[16,128,192]{1,2,0:T(8,128)S(1)}, u32[]{:S(2)}, u32[]{:S(2)}) async-start(f32[16,128,192]{1,2,0:T(8,128)} %broadcast_in_dim.5), calls=%async_computation.2 | async-start | bytes 3145728 | tf_op jit(solution)/shard_map/all_to_all | solution.py:41
Sparse Core Ops, SparseCore 0:
  10.1 34.4 all-gather.3
  46.6 97.3 all-gather.5
  227.7 87.7 all-gather.7
where the time goes:
time: 454 us; the launch traced here: 449 us
  waiting for transfers between devices  231 us (51%)
  blocking collectives  153 us (34%)
  starting transfers between devices  30.4 us (7%)
  matrix products  15.7 us (3%)
  between operations  14.6 us (3%)
    all_gather x2, waiting for transfers between devices, gather_axes(): x = lax.all_gather(x, axis, axis=dim, tiled=True)  136 us
    psum x5, blocking collectives, over_axes(): return functools.reduce(lax.psum, axes, x)  62.2 us
    all_gather x1, waiting for transfers between devices, on_device(): cov_panel = lax.all_gather(cov_tile, GRP, axis=1, tiled=True)  61.1 us
    all_gather x1, blocking collectives, on_device(): grad_cols = lax.all_gather(weight_grad, MEM, axis=0, tiled=True)  35.8 us
    all_to_all x2, waiting for transfers between devices, sent_to_all(): return lax.all_to_all(copies, axis, split_axis=0, concat_axis=0, tiled=True)  33.2 us
    all_gather x1, blocking collectives, on_device(): next_cols = lax.all_gather(next_tile, MEM, axis=0, tiled=True)  27.9 us
    all_gather x1, blocking collectives, on_device(): first_cols = lax.all_gather(cov_tile, MEM, axis=0, tiled=True)  26.8 us
    all_to_all x2, starting transfers between devices, sent_to_all(): return lax.all_to_all(copies, axis, split_axis=0, concat_axis=0, tiled=True)  19.4 us
  transfers between devices with their start and end apart: 6, of which 4 were waited for; matrix products, arithmetic and copies ran while one was open for 1% of the time, Pallas kernels for 0%

commit v1 on v0

v1 whole, which is shorter than its diff:
```python
import functools

import jax
import jax.numpy as jnp
from jax import lax
from jax.experimental import pallas as pl
from jax.experimental.pallas import tpu as pltpu
from jax.sharding import PartitionSpec as P

MESH = pl.DeviceIdType.MESH
F32 = jnp.float32
BF16 = jnp.bfloat16
CH = 4
ROWS = 128 // CH
rem = lax.rem
div = lax.div


def rcopy(src, dst, ssem, rsem, g, m):
    cp = pltpu.make_async_remote_copy(
        src_ref=src, dst_ref=dst, send_sem=ssem, recv_sem=rsem,
        device_id=(g, m), device_id_type=MESH,
    )
    cp.start()


def wait_bytes(ref, sem):
    pltpu.make_async_copy(ref, ref, sem).wait()


def wait_some(ref, sem, fewer):
    @pl.when(fewer)
    def _():
        wait_bytes(ref.at[pl.ds(0, ref.shape[0] - 1)], sem)

    @pl.when(jnp.logical_not(fewer))
    def _():
        wait_bytes(ref, sem)


def kernel(
    x_hbm, w_hbm, root_ref, cond_ref,
    xb, wv, sb, rb, ss, sso, ssx, ssb, yb, rowp, colp, exs, exr,
    ab, bb, rowp2, colp2, exs2, exr2, zb, zx, zp, wp, cxs, cxr,
    lsem, ag_send, ag_recv, fw_send, fw_recv, ss_sem, rs_send, rs_recv,
    sr_send, sr_recv, row_send, row_recv, col_send, col_recv, ex_send, ex_recv,
    w_send, w_recv,
):
    g = lax.axis_index("grp")
    m = lax.axis_index("mem")
    k, c = rem(g, 2), div(g, 2)
    z, xh = div(c, 2), rem(c, 2)
    y, xl = div(m, 2), rem(m, 2)
    x = 2 * xh + xl
    role = rem(x + 2 * y + z, 4)
    partner = c * 2 + 1 - k

    def place(xx, yy, zz, kk):
        return (zz * 2 + div(xx, 2)) * 2 + kk, yy * 2 + rem(xx, 2)

    own = 4 * k
    load_x = pltpu.make_async_copy(x_hbm, xb.at[pl.ds(own * 128, 128)], lsem.at[0])
    load_w = pltpu.make_async_copy(w_hbm, wv, lsem.at[1])
    load_x.start()
    load_w.start()

    def rows(slot, ch):
        return pl.ds(pl.multiple_of(slot * 128 + ch * ROWS, ROWS), ROWS)

    load_x.wait()
    near = (
        place(rem(x + 1 - k, 4), y, rem(z + k, 8), k),
        place(rem(x + 3 * (1 - k), 4), y, rem(z + 7 * k, 8), k),
        place(x, rem(y + 1 + 6 * k, 8), z, k),
    )
    for ch in range(CH):
        for j in range(3):
            rcopy(xb.at[rows(own, ch)], xb.at[rows(own + 1 + j, ch)],
                  ag_send, ag_recv.at[j, ch], *near[j])
    whole = pl.ds(pl.multiple_of(own * 128, 128), 128)
    rcopy(xb.at[whole], xb.at[whole], fw_send, fw_recv, partner, m)

    def squares(r):
        v = xb[r, :].astype(F32)
        s = jnp.sum(v * v, axis=0, keepdims=True)
        t = s[:, 0:128]
        for i in range(1, 16):
            t = t + s[:, i * 128:(i + 1) * 128]
        return t

    total = jnp.zeros((1, 128), F32)
    for ch in range(CH):
        total = total + squares(rows(own, ch))
    for ch in range(CH):
        for j in range(3):
            r = rows(own + 1 + j, ch)
            wait_bytes(xb.at[r], ag_recv.at[j, ch])
            rcopy(xb.at[r], xb.at[r], fw_send, fw_recv, partner, m)
            total = total + squares(r)
    ss[...] = total
    rcopy(ss, sso, ss_sem.at[0], ss_sem.at[1], partner, m)
    wait_bytes(xb.at[pl.ds(0, 512)], fw_recv)
    wait_bytes(sso, ss_sem.at[1])
    ssx[...] = ss[...] + sso[...]

    def cols(i):
        return xb[:, pl.ds(pl.multiple_of(i * 128, 128), 128)]

    @pl.loop(0, 4)
    def _(q):
        m0 = 8 * k + rem(role + 4 - q, 4)
        left = jnp.concatenate([cols(m0), cols(m0 + 4)], axis=1)
        zs = [rem(q, 2) + 2 * t for t in range(4)]
        cs = [2 * zt + rem(div(q + 8 - zt, 2), 2) for zt in zs]
        right = jnp.concatenate([cols(ct) for ct in cs], axis=1)
        part = lax.dot_general(left, right, (((0,), (0,)), ((), ())),
                               preferred_element_type=F32).astype(BF16)
        for a in range(2):
            yy = div(m0 + 4 * a, 2) - 4 * k
            for t in range(4):
                tile = part[a * 128:(a + 1) * 128, t * 128:(t + 1) * 128]
                sb[pl.ds((yy * 8 + zs[t]) * 2, 2)] = tile.reshape(2, 64, 128)

    slot = 8 * y + z

    @pl.loop(0, 32)
    def _(i):
        yo = rem(y + div(i, 8), 4)
        yy = 4 * k + yo
        zz = rem(z + rem(i, 8), 8)
        xx = rem(role + 24 - 2 * yy - zz, 4)
        for half in range(2):
            dg, dm = place(xx, yy, zz, half)
            piece = sb.at[(yo * 8 + zz) * 2 + half]
            mine = jnp.logical_and(dg == g, dm == m)

            @pl.when(mine)
            def _():
                rb[slot] = piece[...]
                ssb[slot] = ssx[...]

            @pl.when(jnp.logical_not(mine))
            def _():
                rcopy(piece, rb.at[slot], rs_send, rs_recv, dg, dm)
                rcopy(ssx, ssb.at[slot], sr_send, sr_recv, dg, dm)

    load_w.wait()
    at_home = div(y, 4) == k
    wait_some(rb, rs_recv, at_home)
    wait_some(ssb, sr_recv, at_home)

    def add8(i, acc):
        for j in range(8):
            acc = acc + rb[i * 8 + j].astype(F32)
        return acc

    cov = lax.fori_loop(0, 8, add8, jnp.zeros((64, 128), F32))
    total_sq = jnp.sum(ssb[...])
    scale = 2048.0 / (6.0 * total_sq)
    it = cov * scale
    row_core, col_core = div(c, 8), div(m, 8)
    row_slot = 2 * rem(c, 8) + k
    col_slot = 2 * rem(m, 8) + k
    own_row, own_col = row_core == k, col_core == k

    def along_row(src, dst, n):
        @pl.loop(0, 16)
        def _(i):
            dg = 2 * rem(c + i, 16) + row_core

            @pl.when(dg == g)
            def _():
                dst[row_slot] = src[...]

            @pl.when(dg != g)
            def _():
                rcopy(src, dst.at[row_slot], row_send.at[n], row_recv.at[n], dg, m)

    def along_col(src, dst, n):
        @pl.loop(0, 16)
        def _(i):
            dg, dm = 2 * c + col_core, rem(m + i, 16)
            mine = jnp.logical_and(dg == g, dm == m)

            @pl.when(mine)
            def _():
                dst[col_slot] = src[...]

            @pl.when(jnp.logical_not(mine))
            def _():
                rcopy(src, dst.at[col_slot], col_send.at[n], col_recv.at[n], dg, dm)

    def spread_w():
        @pl.loop(0, 16)
        def _(i):
            dg, dm = 2 * c + col_core, rem(m + i, 16)
            mine = jnp.logical_and(dg == g, dm == m)

            @pl.when(mine)
            def _():
                wp[col_slot] = wv[...]

            @pl.when(jnp.logical_not(mine))
            def _():
                rcopy(wv, wp.at[col_slot], w_send, w_recv, dg, dm)

    def side_by_side(ref):
        return jnp.concatenate(
            [ref[2 * j:2 * j + 2].reshape(128, 128) for j in range(8)], axis=1)

    def tile_product(lp, rp, out, got, n):
        out[...] = jnp.dot(side_by_side(lp), rp[...].reshape(1024, 128),
                           preferred_element_type=F32)
        other = pl.ds(pl.multiple_of(64 * (1 - k), 64), 64)
        rcopy(out.at[other], got, ex_send.at[n], ex_recv.at[n], partner, m)
        mine = out[pl.ds(pl.multiple_of(64 * k, 64), 64), :]
        wait_bytes(got, ex_recv.at[n])
        return mine + got[...]

    yb[...] = it.astype(BF16)
    along_row(yb, rowp, 0)
    along_col(yb, colp, 0)
    spread_w()
    wait_some(rowp, row_recv.at[0], own_row)
    wait_some(colp, col_recv.at[0], own_col)
    sq = tile_product(rowp, colp, exs, exr, 0)

    ab[...] = sq.astype(BF16)
    bb[...] = (0.0625 * sq - 0.5625 * it).astype(BF16)
    along_row(ab, rowp2, 1)
    along_col(bb, colp2, 1)
    wait_some(rowp2, row_recv.at[1], own_row)
    wait_some(colp2, col_recv.at[1], own_col)
    higher = tile_product(rowp2, colp2, exs2, exr2, 1)

    row_ids = m * 128 + 64 * k + lax.broadcasted_iota(jnp.int32, (64, 128), 0)
    col_ids = c * 128 + lax.broadcasted_iota(jnp.int32, (64, 128), 1)
    unit = jnp.where(row_ids == col_ids, 2.25, 0.0).astype(F32)
    zz_tile = unit - 2.4375 * it + 1.6875 * sq + higher
    zb[...] = zz_tile
    along_row(zb, zp, 2)
    rcopy(zb, zx, ex_send.at[2], ex_recv.at[2], partner, m)

    def half_lanes(v):
        return jnp.where(k == 0, v[:, :64], v[:, 64:])

    root_ref[pl.ds(pl.multiple_of(64 * k, 64), 64), :] = half_lanes(zz_tile)
    wait_bytes(zx, ex_recv.at[2])
    root_ref[pl.ds(pl.multiple_of(64 * (1 - k), 64), 64), :] = half_lanes(zx[...])

    wait_some(wp, w_recv, own_col)
    wait_some(zp, row_recv.at[2], own_row)
    left = side_by_side(zp)
    hi = left.astype(BF16)
    lo = (left - hi.astype(F32)).astype(BF16)

    def weighted(kk):
        right = jnp.concatenate([wp[2 * j + kk] for j in range(8)], axis=0)
        return (jnp.dot(hi, right, preferred_element_type=F32)
                + jnp.dot(lo, right, preferred_element_type=F32))

    cxs[...] = weighted(1 - k)
    rcopy(cxs, cxr, ex_send.at[3], ex_recv.at[3], partner, m)
    out = weighted(k)
    wait_bytes(cxr, ex_recv.at[3])
    cond_ref[...] = out + cxr[...]

    wait_bytes(xb.at[pl.ds(0, 384)], ag_send)
    wait_bytes(xb.at[pl.ds(0, 512)], fw_send)
    wait_bytes(ss, ss_sem.at[0])
    wait_some(sb, rs_send, at_home)
    wait_some(ssb, sr_send, at_home)
    wait_some(rowp, row_send.at[0], own_row)
    wait_some(colp, col_send.at[0], own_col)
    wait_some(rowp2, row_send.at[1], own_row)
    wait_some(colp2, col_send.at[1], own_col)
    wait_some(zp, row_send.at[2], own_row)
    wait_some(wp, w_send, own_col)
    wait_bytes(exr, ex_send.at[0])
    wait_bytes(exr2, ex_send.at[1])
    wait_bytes(zx, ex_send.at[2])
    wait_bytes(cxr, ex_send.at[3])


def on_device(hidden_grads, weight_grad):
    dma = pltpu.SemaphoreType.DMA
    vm = pltpu.VMEM
    return pl.pallas_call(
        kernel,
        out_shape=(jax.ShapeDtypeStruct((128, 64), F32), jax.ShapeDtypeStruct((128, 192), F32)),
        in_specs=[pl.BlockSpec(memory_space=pl.ANY)] * 2,
        out_specs=(pl.BlockSpec(memory_space=pltpu.VMEM),) * 2,
        scratch_shapes=[
            vm((1024, 2048), BF16),
            vm((128, 192), BF16),
            vm((64, 64, 128), BF16),
            vm((64, 64, 128), BF16),
            vm((1, 128), F32), vm((1, 128), F32), vm((1, 128), F32),
            vm((64, 1, 128), F32),
            vm((64, 128), BF16),
            vm((16, 64, 128), BF16), vm((16, 64, 128), BF16),
            vm((128, 128), F32), vm((64, 128), F32),
            vm((64, 128), BF16), vm((64, 128), BF16),
            vm((16, 64, 128), BF16), vm((16, 64, 128), BF16),
            vm((128, 128), F32), vm((64, 128), F32),
            vm((64, 128), F32), vm((64, 128), F32),
            vm((16, 64, 128), F32),
            vm((16, 128, 192), BF16),
            vm((128, 192), F32), vm((128, 192), F32),
            dma((2,)), dma, dma((3, CH)), dma, dma, dma((2,)), dma, dma,
            dma, dma, dma((3,)), dma((3,)), dma((2,)), dma((2,)), dma((4,)), dma((4,)),
            dma, dma,
        ],
        compiler_params=pltpu.CompilerParams(has_side_effects=True, vmem_limit_bytes=48 * 1024 * 1024),
        name="kfac",
    )(hidden_grads, weight_grad)


def solution(mesh):
    spec = P("mem", "grp")
    return jax.shard_map(
        on_device,
        mesh=mesh,
        in_specs=(P(("grp", "mem"), None), spec),
        out_specs=(spec, spec),
        check_vma=False,
    )
```

time: 454 us -> 157 us (0.35); the launches traced: 449 us -> 156 us
  waiting for transfers between devices: 231 us -> 0 us
  blocking collectives: 153 us -> 0 us
  Pallas kernels: 0 us -> 152 us
  starting transfers between devices: 30.4 us -> 0 us
  matrix products: 15.7 us -> 0 us
  between operations: 14.6 us -> 0.65 us
    all_gather x3 -> x0, waiting for transfers between devices: 197 us -> none  [the longest x2 136 us: gather_axes(): x = lax.all_gather(x, axis, axis=dim, tiled=True)]
    pallas_call x0 -> x1, Pallas kernels: none -> 152 us  [on_device(): pl.pallas_call(kernel, out_shape=(jax.ShapeDtypeStruct((128, 64), F32), j...]
    all_gather x3 -> x0, blocking collectives: 90.5 us -> none  [the longest x1 35.8 us: on_device(): grad_cols = lax.all_gather(weight_grad, MEM, axis=0, tiled=True)]
    psum x5 -> x0, blocking collectives: 62.2 us -> none  [over_axes(): return functools.reduce(lax.psum, axes, x)]
    all_to_all x3 -> x0, waiting for transfers between devices: 33.2 us -> none  [the longest x2 33.2 us: sent_to_all(): return lax.all_to_all(copies, axis, split_axis=0, concat_axis=0, tiled=True)]
    all_to_all x3 -> x0, starting transfers between devices: 30.3 us -> none  [the longest x2 19.4 us: sent_to_all(): return lax.all_to_all(copies, axis, split_axis=0, concat_axis=0, tiled=True)]
    dot_general x6 -> x0, matrix products: 15.7 us -> none  [the longest x1 8.02 us: on_device(): lax.dot_general(own_cols, block_rows, (((0,), (0,)), ((), ())), preferred...]
  transfers between devices with their start and end apart: 6 -> 0, of which waited for: 4 -> 0; matrix products, arithmetic and copies ran while one was open for 1% -> 0% of each run, Pallas kernels for 0% -> 0%
where the time goes in v1:
time: 157 us; the launch traced here: 156 us
  Pallas kernels  152 us (97%)
  local copies, waits for them, and re-layouts  3.37 us (2%)
    pallas_call x1, Pallas kernels, on_device(): pl.pallas_call(kernel, out_shape=(jax.ShapeDtypeStruct((128, 64), F32), j...  152 us

profile of v1, /device:TPU:1, one launch (start us, length us, event | category | flops | bytes accessed | tf_op | source)
XLA Modules:
  0.0 156.3 jit_solution(5450157222894279045)
XLA Ops:
  0.6 0.9 copy.4.w_hbm
  1.5 0.0 copy-start
  1.5 1.0 copy-done
  2.6 152.3 %kfac.1 = (f32[128,64]{1,0:T(8,128)S(1)}, f32[128,192]{1,0:T(8,128)S(1)}) custom-call(bf16[128,2048]{1,0:T(8,128)(2,1)S(1)} %copy-done, bf16[128,192]{1,0:T(8,128)(2,1)S(1)} %copy.4.w_hbm), custom_call_target="tpu_custom_call" | custom-call | tf_op jit(solution)/shard_map/kfac/pallas_call | solution.py:288
  154.9 0.7 copy.5
  155.6 0.7 copy.6
Async XLA Ops:
  1.5 1.0 copy-start

commit v2 on v1

--- a/solution.py
+++ b/solution.py
@@ -40,9 +40,9 @@
 
 def kernel(
     x_hbm, w_hbm, root_ref, cond_ref,
-    xb, wv, sb, rb, ss, sso, ssx, ssb, yb, rowp, colp, exs, exr,
-    ab, bb, rowp2, colp2, exs2, exr2, zb, zx, zp, wp, cxs, cxr,
-    lsem, ag_send, ag_recv, fw_send, fw_recv, ss_sem, rs_send, rs_recv,
+    xb, wv, sb, ra, sb2, rb, ss, sso, ssx, ssa, ssy, ssb, yb, rowp, colp, exs, exr,
+    ab, bb, rowp2, colp2, exs2, exr2, zb, zx, qb, qp, wp, cxs, cxr,
+    lsem, ag_send, ag_recv, fw_send, fw_recv, ss_sem, rs_send, rs_recv, rs2_send, rs2_recv,
     sr_send, sr_recv, row_send, row_recv, col_send, col_recv, ex_send, ex_recv,
     w_send, w_recv,
 ):
@@ -64,8 +64,38 @@
     load_x.start()
     load_w.start()
 
+    barrier = pltpu.get_barrier_semaphore()
+
+    def greet(dg, dm):
+        pl.semaphore_signal(barrier, inc=1, device_id=(dg, dm), device_id_type=MESH)
+
+    def diagonal(dy, dz):
+        yy, zz = rem(y + dy, 8), rem(z + dz, 8)
+        return rem(role + 24 - 2 * yy - zz, 4), yy, zz
+
+    greet(partner, m)
+    for step in (1, 7):
+        greet(*place(rem(x + step * (1 - k), 4), y, rem(z + step * k, 8), k))
+        greet(*place(x, rem(y + step, 8), z, k))
+
+    @pl.loop(1, 8)
+    def _(i):
+        for half in range(2):
+            greet(*place(*diagonal(i, 0), half))
+            greet(*place(*diagonal(0, i), half))
+
+    @pl.loop(1, 16)
+    def _(i):
+        for half in range(2):
+            greet(2 * rem(c + i, 16) + half, m)
+            greet(2 * c + half, rem(m + i, 16))
+
+    pl.semaphore_wait(barrier, 5 + 28 + 60)
+
     def rows(slot, ch):
         return pl.ds(pl.multiple_of(slot * 128 + ch * ROWS, ROWS), ROWS)
+
+    pending = []
 
     load_x.wait()
     near = (
@@ -79,6 +109,28 @@
                   ag_send, ag_recv.at[j, ch], *near[j])
     whole = pl.ds(pl.multiple_of(own * 128, 128), 128)
     rcopy(xb.at[whole], xb.at[whole], fw_send, fw_recv, partner, m)
+    pending.append(lambda: wait_bytes(xb.at[pl.ds(0, 384)], ag_send))
+    pending.append(lambda: wait_bytes(xb.at[pl.ds(0, 512)], fw_send))
+
+    load_w.wait()
+    w_slot = 8 * xl + 2 * rem(y, 4) + k
+    w_core = div(y, 4)
+    w_kept = w_core == k
+
+    @pl.loop(1, 9)
+    def _(i):
+        mine = jnp.logical_and(i == 8, w_kept)
+
+        @pl.when(mine)
+        def _():
+            wp[w_slot] = wv[...]
+
+        @pl.when(jnp.logical_not(mine))
+        def _():
+            rcopy(wv, wp.at[w_slot], w_send.at[0], w_recv.at[0], *place(x, rem(y + i, 8), z, w_core))
+
+    w_mine = pl.ds(8 * xl, 8)
+    pending.append(lambda: wait_some(wp.at[pl.ds(0, 8)], w_send.at[0], w_kept))
 
     def squares(r):
         v = xb[r, :].astype(F32)
@@ -99,6 +151,7 @@
             total = total + squares(r)
     ss[...] = total
     rcopy(ss, sso, ss_sem.at[0], ss_sem.at[1], partner, m)
+    pending.append(lambda: wait_bytes(ss, ss_sem.at[0]))
     wait_bytes(xb.at[pl.ds(0, 512)], fw_recv)
     wait_bytes(sso, ss_sem.at[1])
     ssx[...] = ss[...] + sso[...]
@@ -116,45 +169,107 @@
         part = lax.dot_general(left, right, (((0,), (0,)), ((), ())),
                                preferred_element_type=F32).astype(BF16)
         for a in range(2):
-            yy = div(m0 + 4 * a, 2) - 4 * k
+            yo = div(m0 + 4 * a, 2) - 4 * k
             for t in range(4):
                 tile = part[a * 128:(a + 1) * 128, t * 128:(t + 1) * 128]
-                sb[pl.ds((yy * 8 + zs[t]) * 2, 2)] = tile.reshape(2, 64, 128)
-
-    slot = 8 * y + z
-
-    @pl.loop(0, 32)
-    def _(i):
-        yo = rem(y + div(i, 8), 4)
+                sb[0, zs[t] * 4 + yo] = tile[:64]
+                sb[1, yo * 8 + zs[t]] = tile[64:]
+
+    first_slot = z * (1 - k) + y * k
+    second_slot = y * (1 - k) + z * k
+    in_half = div(y, 4) == k
+    on_low = k == 0
+
+    @pl.loop(1, 9)
+    def _(i):
+        xx, yy, zz = diagonal(0, i)
+        dg, dm = place(xx, yy, zz, 0)
+        piece = sb.at[0, pl.ds(zz * 4, 4)]
+        there = pl.ds(z * 8 + 4 * k, 4)
+        mine = jnp.logical_and(on_low, i == 8)
+
+        @pl.when(mine)
+        def _():
+            ra[there] = piece[...]
+
+        @pl.when(jnp.logical_not(mine))
+        def _():
+            rcopy(piece, ra.at[there], rs_send.at[0], rs_recv, dg, dm)
+
+    @pl.loop(1, 5)
+    def _(i):
+        yo = rem(y + i, 4)
         yy = 4 * k + yo
-        zz = rem(z + rem(i, 8), 8)
-        xx = rem(role + 24 - 2 * yy - zz, 4)
-        for half in range(2):
-            dg, dm = place(xx, yy, zz, half)
-            piece = sb.at[(yo * 8 + zz) * 2 + half]
-            mine = jnp.logical_and(dg == g, dm == m)
-
-            @pl.when(mine)
-            def _():
-                rb[slot] = piece[...]
-                ssb[slot] = ssx[...]
-
-            @pl.when(jnp.logical_not(mine))
-            def _():
-                rcopy(piece, rb.at[slot], rs_send, rs_recv, dg, dm)
-                rcopy(ssx, ssb.at[slot], sr_send, sr_recv, dg, dm)
-
-    load_w.wait()
-    at_home = div(y, 4) == k
-    wait_some(rb, rs_recv, at_home)
-    wait_some(ssb, sr_recv, at_home)
-
-    def add8(i, acc):
-        for j in range(8):
-            acc = acc + rb[i * 8 + j].astype(F32)
-        return acc
-
-    cov = lax.fori_loop(0, 8, add8, jnp.zeros((64, 128), F32))
+        xx = rem(role + 24 - 2 * yy - z, 4)
+        dg, dm = place(xx, yy, z, 1)
+        piece = sb.at[1, pl.ds(yo * 8, 8)]
+        there = pl.ds(y * 8, 8)
+        mine = jnp.logical_and(k == 1, yy == y)
+
+        @pl.when(mine)
+        def _():
+            ra[there] = piece[...]
+
+        @pl.when(jnp.logical_not(mine))
+        def _():
+            rcopy(piece, ra.at[there], rs_send.at[1], rs_recv, dg, dm)
+
+    wait_some(wp.at[pl.ds(0, 8)], w_recv.at[0], w_kept)
+    rcopy(wp.at[w_mine], wp.at[w_mine], w_send.at[1], w_recv.at[1], *place(2 * xh + 1 - xl, y, z, k))
+    pending.append(lambda: wait_bytes(wp.at[pl.ds(0, 8)], w_send.at[1]))
+    ssa[first_slot] = ssx[...]
+
+    @pl.loop(1, 8)
+    def _(i):
+        dg, dm = place(*diagonal(k * i, (1 - k) * i), k)
+        rcopy(ssx, ssa.at[first_slot], sr_send.at[0], sr_recv.at[0], dg, dm)
+
+    def wait_first(sem, sending):
+        full = sb.at[0]
+        if sending:
+            pl.when(on_low)(lambda: wait_bytes(full.at[pl.ds(0, 28)], sem.at[0]))
+            pl.when(k == 1)(lambda: wait_bytes(full, sem.at[0]))
+            kept = jnp.logical_and(k == 1, in_half)
+            pl.when(kept)(lambda: wait_bytes(full.at[pl.ds(0, 24)], sem.at[1]))
+            pl.when(jnp.logical_not(kept))(lambda: wait_bytes(full, sem.at[1]))
+        else:
+            kept = jnp.logical_and(k == 1, in_half)
+            pl.when(on_low)(lambda: wait_bytes(ra.at[pl.ds(0, 60)], sem))
+            pl.when(kept)(lambda: wait_bytes(ra.at[pl.ds(0, 56)], sem))
+            pl.when(jnp.logical_and(k == 1, jnp.logical_not(in_half)))(lambda: wait_bytes(ra, sem))
+
+    pending.append(lambda: wait_first(rs_send, True))
+    pending.append(lambda: wait_bytes(ssa.at[pl.ds(0, 7)], sr_send.at[0]))
+    wait_first(rs_recv, False)
+    wait_bytes(ssa.at[pl.ds(0, 7)], sr_recv.at[0])
+    ssy[...] = jnp.sum(ssa[...], axis=0)
+
+    @pl.loop(1, 9)
+    def _(i):
+        to = rem(second_slot + i, 8)
+        acc = ra[to].astype(F32)
+        for j in range(1, 8):
+            acc = acc + ra[j * 8 + to].astype(F32)
+        dg, dm = place(*diagonal((1 - k) * i, k * i), k)
+
+        @pl.when(i == 8)
+        def _():
+            rb[second_slot] = acc
+            ssb[second_slot] = ssy[...]
+
+        @pl.when(i < 8)
+        def _():
+            sb2[to] = acc
+            rcopy(sb2.at[to], rb.at[second_slot], rs2_send, rs2_recv, dg, dm)
+            rcopy(ssy, ssb.at[second_slot], sr_send.at[1], sr_recv.at[1], dg, dm)
+
+    pending.append(lambda: wait_bytes(rb.at[pl.ds(0, 7)], rs2_send))
+    pending.append(lambda: wait_bytes(ssb.at[pl.ds(0, 7)], sr_send.at[1]))
+    wait_bytes(rb.at[pl.ds(0, 7)], rs2_recv)
+    wait_bytes(ssb.at[pl.ds(0, 7)], sr_recv.at[1])
+    cov = rb[0]
+    for j in range(1, 8):
+        cov = cov + rb[j]
     total_sq = jnp.sum(ssb[...])
     scale = 2048.0 / (6.0 * total_sq)
     it = cov * scale
@@ -189,20 +304,6 @@
             @pl.when(jnp.logical_not(mine))
             def _():
                 rcopy(src, dst.at[col_slot], col_send.at[n], col_recv.at[n], dg, dm)
-
-    def spread_w():
-        @pl.loop(0, 16)
-        def _(i):
-            dg, dm = 2 * c + col_core, rem(m + i, 16)
-            mine = jnp.logical_and(dg == g, dm == m)
-
-            @pl.when(mine)
-            def _():
-                wp[col_slot] = wv[...]
-
-            @pl.when(jnp.logical_not(mine))
-            def _():
-                rcopy(wv, wp.at[col_slot], w_send, w_recv, dg, dm)
 
     def side_by_side(ref):
         return jnp.concatenate(
@@ -217,29 +318,39 @@
         wait_bytes(got, ex_recv.at[n])
         return mine + got[...]
 
-    yb[...] = it.astype(BF16)
+    it16 = it.astype(BF16)
+    yb[...] = it16
     along_row(yb, rowp, 0)
     along_col(yb, colp, 0)
-    spread_w()
+    pending.append(lambda: wait_some(rowp, row_send.at[0], own_row))
+    pending.append(lambda: wait_some(colp, col_send.at[0], own_col))
     wait_some(rowp, row_recv.at[0], own_row)
     wait_some(colp, col_recv.at[0], own_col)
     sq = tile_product(rowp, colp, exs, exr, 0)
-
-    ab[...] = sq.astype(BF16)
+    pending.append(lambda: wait_bytes(exr, ex_send.at[0]))
+
+    sq16 = sq.astype(BF16)
+    ab[...] = sq16
     bb[...] = (0.0625 * sq - 0.5625 * it).astype(BF16)
     along_row(ab, rowp2, 1)
     along_col(bb, colp2, 1)
+    pending.append(lambda: wait_some(rowp2, row_send.at[1], own_row))
+    pending.append(lambda: wait_some(colp2, col_send.at[1], own_col))
     wait_some(rowp2, row_recv.at[1], own_row)
     wait_some(colp2, col_recv.at[1], own_col)
     higher = tile_product(rowp2, colp2, exs2, exr2, 1)
+    pending.append(lambda: wait_bytes(exr2, ex_send.at[1]))
 
     row_ids = m * 128 + 64 * k + lax.broadcasted_iota(jnp.int32, (64, 128), 0)
     col_ids = c * 128 + lax.broadcasted_iota(jnp.int32, (64, 128), 1)
     unit = jnp.where(row_ids == col_ids, 2.25, 0.0).astype(F32)
     zz_tile = unit - 2.4375 * it + 1.6875 * sq + higher
+    qb[...] = (higher - 2.4375 * (it - it16.astype(F32)) + 1.6875 * (sq - sq16.astype(F32))).astype(BF16)
+    along_row(qb, qp, 2)
     zb[...] = zz_tile
-    along_row(zb, zp, 2)
     rcopy(zb, zx, ex_send.at[2], ex_recv.at[2], partner, m)
+    pending.append(lambda: wait_some(qp, row_send.at[2], own_row))
+    pending.append(lambda: wait_bytes(zx, ex_send.at[2]))
 
     def half_lanes(v):
         return jnp.where(k == 0, v[:, :64], v[:, 64:])
@@ -248,38 +359,31 @@
     wait_bytes(zx, ex_recv.at[2])
     root_ref[pl.ds(pl.multiple_of(64 * (1 - k), 64), 64), :] = half_lanes(zx[...])
 
-    wait_some(wp, w_recv, own_col)
-    wait_some(zp, row_recv.at[2], own_row)
-    left = side_by_side(zp)
+    wait_bytes(wp.at[pl.ds(0, 8)], w_recv.at[1])
+    left = 1.6875 * side_by_side(rowp2).astype(F32) - 2.4375 * side_by_side(rowp).astype(F32)
     hi = left.astype(BF16)
     lo = (left - hi.astype(F32)).astype(BF16)
 
-    def weighted(kk):
-        right = jnp.concatenate([wp[2 * j + kk] for j in range(8)], axis=0)
-        return (jnp.dot(hi, right, preferred_element_type=F32)
-                + jnp.dot(lo, right, preferred_element_type=F32))
-
-    cxs[...] = weighted(1 - k)
+    def right(kk):
+        return jnp.concatenate([wp[8 * (j % 2) + 2 * (j // 2) + kk] for j in range(8)], axis=0)
+
+    def known(kk):
+        return (jnp.dot(hi, right(kk), preferred_element_type=F32)
+                + jnp.dot(lo, right(kk), preferred_element_type=F32))
+
+    cxs[...] = known(1 - k)
+    cond_ref[...] = known(k) + 2.25 * wv[...].astype(F32)
+    wait_some(qp, row_recv.at[2], own_row)
+    rest = side_by_side(qp)
+    cxs[...] += jnp.dot(rest, right(1 - k), preferred_element_type=F32)
     rcopy(cxs, cxr, ex_send.at[3], ex_recv.at[3], partner, m)
-    out = weighted(k)
+    pending.append(lambda: wait_bytes(cxr, ex_send.at[3]))
+    cond_ref[...] += jnp.dot(rest, right(k), preferred_element_type=F32)
     wait_bytes(cxr, ex_recv.at[3])
-    cond_ref[...] = out + cxr[...]
-
-    wait_bytes(xb.at[pl.ds(0, 384)], ag_send)
-    wait_bytes(xb.at[pl.ds(0, 512)], fw_send)
-    wait_bytes(ss, ss_sem.at[0])
-    wait_some(sb, rs_send, at_home)
-    wait_some(ssb, sr_send, at_home)
-    wait_some(rowp, row_send.at[0], own_row)
-    wait_some(colp, col_send.at[0], own_col)
-    wait_some(rowp2, row_send.at[1], own_row)
-    wait_some(colp2, col_send.at[1], own_col)
-    wait_some(zp, row_send.at[2], own_row)
-    wait_some(wp, w_send, own_col)
-    wait_bytes(exr, ex_send.at[0])
-    wait_bytes(exr2, ex_send.at[1])
-    wait_bytes(zx, ex_send.at[2])
-    wait_bytes(cxr, ex_send.at[3])
+    cond_ref[...] += cxr[...]
+
+    for finish in pending:
+        finish()
 
 
 def on_device(hidden_grads, weight_grad):
@@ -293,10 +397,11 @@
         scratch_shapes=[
             vm((1024, 2048), BF16),
             vm((128, 192), BF16),
+            vm((2, 32, 64, 128), BF16),
             vm((64, 64, 128), BF16),
-            vm((64, 64, 128), BF16),
+            vm((8, 64, 128), F32), vm((8, 64, 128), F32),
             vm((1, 128), F32), vm((1, 128), F32), vm((1, 128), F32),
-            vm((64, 1, 128), F32),
+            vm((8, 1, 128), F32), vm((1, 128), F32), vm((8, 1, 128), F32),
             vm((64, 128), BF16),
             vm((16, 64, 128), BF16), vm((16, 64, 128), BF16),
             vm((128, 128), F32), vm((64, 128), F32),
@@ -304,14 +409,14 @@
             vm((16, 64, 128), BF16), vm((16, 64, 128), BF16),
             vm((128, 128), F32), vm((64, 128), F32),
             vm((64, 128), F32), vm((64, 128), F32),
-            vm((16, 64, 128), F32),
+            vm((64, 128), BF16), vm((16, 64, 128), BF16),
             vm((16, 128, 192), BF16),
             vm((128, 192), F32), vm((128, 192), F32),
-            dma((2,)), dma, dma((3, CH)), dma, dma, dma((2,)), dma, dma,
-            dma, dma, dma((3,)), dma((3,)), dma((2,)), dma((2,)), dma((4,)), dma((4,)),
-            dma, dma,
+            dma((2,)), dma, dma((3, CH)), dma, dma, dma((2,)), dma((2,)), dma,
+            dma, dma, dma((2,)), dma((2,)), dma((3,)), dma((3,)), dma((2,)), dma((2,)), dma((4,)), dma((4,)),
+            dma((2,)), dma((2,)),
         ],
-        compiler_params=pltpu.CompilerParams(has_side_effects=True, vmem_limit_bytes=48 * 1024 * 1024),
+        compiler_params=pltpu.CompilerParams(has_side_effects=True, collective_id=0, vmem_limit_bytes=48 * 1024 * 1024),
         name="kfac",
     )(hidden_grads, weight_grad)
 

time: 157 us -> 94.6 us (0.60)
  Pallas kernels: 152 us -> 90.4 us
    pallas_call x1, Pallas kernels: 152 us -> 90.4 us  [on_device(): pl.pallas_call(kernel, out_shape=(jax.ShapeDtypeStruct((128, 64), F32), j...]
where the time goes in v2:
time: 94.6 us; the launch traced here: 94.4 us
  Pallas kernels  90.4 us (96%)
  local copies, waits for them, and re-layouts  3.37 us (4%)
    pallas_call x1, Pallas kernels, on_device(): pl.pallas_call(kernel, out_shape=(jax.ShapeDtypeStruct((128, 64), F32), j...  90.4 us
    unnamed x3, local copies, waits for them, and re-layouts  1.93 us

profile of v2, /device:TPU:1, one launch (start us, length us, event | category | flops | bytes accessed | tf_op | source)
XLA Modules:
  0.0 94.4 jit_solution(16858105125920570620)
XLA Ops:
  0.6 0.9 copy.4.w_hbm
  1.5 0.0 copy-start
  1.5 1.0 %copy-done = bf16[128,2048]{1,0:T(8,128)(2,1)S(1)} copy-done((bf16[128,2048]{1,0:T(8,128)(2,1)S(1)}, bf16[128,2048]{1,0:T(8,128)(2,1)}, u32[]{:S(2)}) %copy-start) | copy-done | bytes 524312
  2.6 90.4 %kfac.1 = (f32[128,64]{1,0:T(8,128)S(1)}, f32[128,192]{1,0:T(8,128)S(1)}) custom-call(bf16[128,2048]{1,0:T(8,128)(2,1)S(1)} %copy-done, bf16[128,192]{1,0:T(8,128)(2,1)S(1)} %copy.4.w_hbm), custom_call_target="tpu_custom_call" | custom-call | tf_op jit(solution)/shard_map/kfac/pallas_call | solution.py:392
  93.0 0.7 copy.5
  93.7 0.7 copy.6
Async XLA Ops:
  1.5 1.0 %copy-start = (bf16[128,2048]{1,0:T(8,128)(2,1)S(1)}, bf16[128,2048]{1,0:T(8,128)(2,1)}, u32[]{:S(2)}) copy-start(bf16[128,2048]{1,0:T(8,128)(2,1)} %x_hbm.1) | copy-start | bytes 1572868

commit v3 on v2

--- a/solution.py
+++ b/solution.py
@@ -41,10 +41,10 @@
 def kernel(
     x_hbm, w_hbm, root_ref, cond_ref,
     xb, wv, sb, ra, sb2, rb, ss, sso, ssx, ssa, ssy, ssb, yb, rowp, colp, exs, exr,
-    ab, bb, rowp2, colp2, exs2, exr2, zb, zx, qb, qp, wp, cxs, cxr,
+    ab, bb, rowp2, colp2, exs2, exr2, zb, zx, whole_tile, qb, qp, wp, cxs, cxr,
     lsem, ag_send, ag_recv, fw_send, fw_recv, ss_sem, rs_send, rs_recv, rs2_send, rs2_recv,
     sr_send, sr_recv, row_send, row_recv, col_send, col_recv, ex_send, ex_recv,
-    w_send, w_recv,
+    w_send, w_recv, met,
 ):
     g = lax.axis_index("grp")
     m = lax.axis_index("mem")
@@ -75,25 +75,32 @@
 
     greet(partner, m)
     for step in (1, 7):
-        greet(*place(rem(x + step * (1 - k), 4), y, rem(z + step * k, 8), k))
+        greet(*place(rem(x + step, 4), y, z, k))
         greet(*place(x, rem(y + step, 8), z, k))
-
-    @pl.loop(1, 8)
-    def _(i):
-        for half in range(2):
-            greet(*place(*diagonal(i, 0), half))
-            greet(*place(*diagonal(0, i), half))
-
-    @pl.loop(1, 16)
-    def _(i):
-        for half in range(2):
-            greet(2 * rem(c + i, 16) + half, m)
-            greet(2 * c + half, rem(m + i, 16))
-
-    pl.semaphore_wait(barrier, 5 + 28 + 60)
+        greet(*place(x, y, rem(z + step, 8), k))
+    pl.semaphore_wait(barrier, 7)
+
+    def introduce():
+        def nudge(n, dg, dm):
+            pl.semaphore_signal(met.at[n], inc=1, device_id=(dg, dm), device_id_type=MESH)
+
+        for step in (1, 3):
+            nudge(0, *place(rem(x + step, 4), y, z, k))
+        pl.semaphore_wait(met.at[0], 2)
+        for n, steps in ((1, (1, 7)), (2, (2, 6))):
+            for step in steps:
+                nudge(n, *place(x, rem(y + step, 8), z, k))
+                nudge(n, *place(x, y, rem(z + step, 8), k))
+            pl.semaphore_wait(met.at[n], 4)
+        nudge(3, partner, m)
+        pl.semaphore_wait(met.at[3], 1)
 
     def rows(slot, ch):
         return pl.ds(pl.multiple_of(slot * 128 + ch * ROWS, ROWS), ROWS)
+
+    def diagonal(dy, dz):
+        yy, zz = rem(y + dy, 8), rem(z + dz, 8)
+        return rem(role + 24 - 2 * yy - zz, 4), yy, zz
 
     pending = []
 
@@ -117,19 +124,25 @@
     w_core = div(y, 4)
     w_kept = w_core == k
 
-    @pl.loop(1, 9)
-    def _(i):
-        mine = jnp.logical_and(i == 8, w_kept)
-
-        @pl.when(mine)
-        def _():
-            wp[w_slot] = wv[...]
-
-        @pl.when(jnp.logical_not(mine))
-        def _():
-            rcopy(wv, wp.at[w_slot], w_send.at[0], w_recv.at[0], *place(x, rem(y + i, 8), z, w_core))
-
-    w_mine = pl.ds(8 * xl, 8)
+    def spread_w():
+        @pl.loop(1, 9)
+        def _(i):
+            mine = jnp.logical_and(i == 8, w_kept)
+
+            @pl.when(mine)
+            def _():
+                wp[w_slot] = wv[...]
+
+            @pl.when(jnp.logical_not(mine))
+            def _():
+                rcopy(wv, wp.at[w_slot], w_send.at[0], w_recv.at[0], *place(x, rem(y + i, 8), z, w_core))
+
+    def cross_w(n):
+        some = wp.at[pl.ds(8 * xl + 4 * n, 4)]
+        rcopy(some, some, w_send.at[1], w_recv.at[1], *place(2 * xh + 1 - xl, y, z, k))
+
+    introduce()
+    spread_w()
     pending.append(lambda: wait_some(wp.at[pl.ds(0, 8)], w_send.at[0], w_kept))
 
     def squares(r):
@@ -148,53 +161,56 @@
             r = rows(own + 1 + j, ch)
             wait_bytes(xb.at[r], ag_recv.at[j, ch])
             rcopy(xb.at[r], xb.at[r], fw_send, fw_recv, partner, m)
-            total = total + squares(r)
+        for j in range(3):
+            total = total + squares(rows(own + 1 + j, ch))
     ss[...] = total
     rcopy(ss, sso, ss_sem.at[0], ss_sem.at[1], partner, m)
     pending.append(lambda: wait_bytes(ss, ss_sem.at[0]))
     wait_bytes(xb.at[pl.ds(0, 512)], fw_recv)
-    wait_bytes(sso, ss_sem.at[1])
-    ssx[...] = ss[...] + sso[...]
 
     def cols(i):
         return xb[:, pl.ds(pl.multiple_of(i * 128, 128), 128)]
-
-    @pl.loop(0, 4)
-    def _(q):
-        m0 = 8 * k + rem(role + 4 - q, 4)
-        left = jnp.concatenate([cols(m0), cols(m0 + 4)], axis=1)
-        zs = [rem(q, 2) + 2 * t for t in range(4)]
-        cs = [2 * zt + rem(div(q + 8 - zt, 2), 2) for zt in zs]
-        right = jnp.concatenate([cols(ct) for ct in cs], axis=1)
-        part = lax.dot_general(left, right, (((0,), (0,)), ((), ())),
-                               preferred_element_type=F32).astype(BF16)
-        for a in range(2):
-            yo = div(m0 + 4 * a, 2) - 4 * k
-            for t in range(4):
-                tile = part[a * 128:(a + 1) * 128, t * 128:(t + 1) * 128]
-                sb[0, zs[t] * 4 + yo] = tile[:64]
-                sb[1, yo * 8 + zs[t]] = tile[64:]
 
     first_slot = z * (1 - k) + y * k
     second_slot = y * (1 - k) + z * k
     in_half = div(y, 4) == k
     on_low = k == 0
 
-    @pl.loop(1, 9)
-    def _(i):
-        xx, yy, zz = diagonal(0, i)
-        dg, dm = place(xx, yy, zz, 0)
-        piece = sb.at[0, pl.ds(zz * 4, 4)]
-        there = pl.ds(z * 8 + 4 * k, 4)
-        mine = jnp.logical_and(on_low, i == 8)
-
-        @pl.when(mine)
-        def _():
-            ra[there] = piece[...]
-
-        @pl.when(jnp.logical_not(mine))
-        def _():
-            rcopy(piece, ra.at[there], rs_send.at[0], rs_recv, dg, dm)
+    @pl.loop(0, 2)
+    def _(parity):
+        @pl.loop(0, 2)
+        def _(turn):
+            q = parity + 2 * turn
+            m0 = 8 * k + rem(role + 4 - q, 4)
+            left = jnp.concatenate([cols(m0), cols(m0 + 4)], axis=1)
+            zs = [rem(q, 2) + 2 * t for t in range(4)]
+            cs = [2 * zt + rem(div(q + 8 - zt, 2), 2) for zt in zs]
+            right = jnp.concatenate([cols(ct) for ct in cs], axis=1)
+            part = lax.dot_general(left, right, (((0,), (0,)), ((), ())),
+                                   preferred_element_type=F32).astype(BF16)
+            for a in range(2):
+                yo = div(m0 + 4 * a, 2) - 4 * k
+                for t in range(4):
+                    tile = part[a * 128:(a + 1) * 128, t * 128:(t + 1) * 128]
+                    sb[0, zs[t] * 4 + yo] = tile[:64]
+                    sb[1, yo * 8 + zs[t]] = tile[64:]
+
+        @pl.loop(1, 9)
+        def _(i):
+            xx, yy, zz = diagonal(0, i)
+            dg, dm = place(xx, yy, zz, 0)
+            piece = sb.at[0, pl.ds(zz * 4, 4)]
+            there = pl.ds(z * 8 + 4 * k, 4)
+            ready = rem(zz, 2) == parity
+            mine = jnp.logical_and(ready, jnp.logical_and(on_low, i == 8))
+
+            @pl.when(mine)
+            def _():
+                ra[there] = piece[...]
+
+            @pl.when(jnp.logical_and(ready, jnp.logical_not(jnp.logical_and(on_low, i == 8))))
+            def _():
+                rcopy(piece, ra.at[there], rs_send.at[0], rs_recv, dg, dm)
 
     @pl.loop(1, 5)
     def _(i):
@@ -214,9 +230,8 @@
         def _():
             rcopy(piece, ra.at[there], rs_send.at[1], rs_recv, dg, dm)
 
-    wait_some(wp.at[pl.ds(0, 8)], w_recv.at[0], w_kept)
-    rcopy(wp.at[w_mine], wp.at[w_mine], w_send.at[1], w_recv.at[1], *place(2 * xh + 1 - xl, y, z, k))
-    pending.append(lambda: wait_bytes(wp.at[pl.ds(0, 8)], w_send.at[1]))
+    wait_bytes(sso, ss_sem.at[1])
+    ssx[...] = ss[...] + sso[...]
     ssa[first_slot] = ssx[...]
 
     @pl.loop(1, 8)
@@ -322,6 +337,8 @@
     yb[...] = it16
     along_row(yb, rowp, 0)
     along_col(yb, colp, 0)
+    wait_some(wp.at[pl.ds(0, 8)], w_recv.at[0], w_kept)
+    cross_w(0)
     pending.append(lambda: wait_some(rowp, row_send.at[0], own_row))
     pending.append(lambda: wait_some(colp, col_send.at[0], own_col))
     wait_some(rowp, row_recv.at[0], own_row)
@@ -334,6 +351,8 @@
     bb[...] = (0.0625 * sq - 0.5625 * it).astype(BF16)
     along_row(ab, rowp2, 1)
     along_col(bb, colp2, 1)
+    cross_w(1)
+    pending.append(lambda: wait_bytes(wp.at[pl.ds(0, 8)], w_send.at[1]))
     pending.append(lambda: wait_some(rowp2, row_send.at[1], own_row))
     pending.append(lambda: wait_some(colp2, col_send.at[1], own_col))
     wait_some(rowp2, row_recv.at[1], own_row)
@@ -352,33 +371,31 @@
     pending.append(lambda: wait_some(qp, row_send.at[2], own_row))
     pending.append(lambda: wait_bytes(zx, ex_send.at[2]))
 
-    def half_lanes(v):
-        return jnp.where(k == 0, v[:, :64], v[:, 64:])
-
-    root_ref[pl.ds(pl.multiple_of(64 * k, 64), 64), :] = half_lanes(zz_tile)
     wait_bytes(zx, ex_recv.at[2])
-    root_ref[pl.ds(pl.multiple_of(64 * (1 - k), 64), 64), :] = half_lanes(zx[...])
+    whole_tile[pl.ds(pl.multiple_of(64 * k, 64), 64), :] = zb[...]
+    whole_tile[pl.ds(pl.multiple_of(64 * (1 - k), 64), 64), :] = zx[...]
+    whole_tile[...] = whole_tile[...].T
+    root_ref[...] = whole_tile[pl.ds(pl.multiple_of(64 * k, 64), 64), :]
 
     wait_bytes(wp.at[pl.ds(0, 8)], w_recv.at[1])
     left = 1.6875 * side_by_side(rowp2).astype(F32) - 2.4375 * side_by_side(rowp).astype(F32)
     hi = left.astype(BF16)
     lo = (left - hi.astype(F32)).astype(BF16)
 
-    def right(kk):
-        return jnp.concatenate([wp[8 * (j % 2) + 2 * (j // 2) + kk] for j in range(8)], axis=0)
-
-    def known(kk):
-        return (jnp.dot(hi, right(kk), preferred_element_type=F32)
-                + jnp.dot(lo, right(kk), preferred_element_type=F32))
-
-    cxs[...] = known(1 - k)
-    cond_ref[...] = known(k) + 2.25 * wv[...].astype(F32)
+    def weighted(kk, parts):
+        cols_kk = jnp.concatenate(
+            [wp[8 * (j % 2) + 2 * (j // 2) + kk] for j in range(8)], axis=1)
+        return sum(lax.dot_general(cols_kk, p, (((1,), (1,)), ((), ())),
+                                   preferred_element_type=F32) for p in parts)
+
+    cxs[...] = weighted(1 - k, (hi, lo))
+    cond_ref[...] = weighted(k, (hi, lo)) + 2.25 * wv[...].astype(F32)
     wait_some(qp, row_recv.at[2], own_row)
     rest = side_by_side(qp)
-    cxs[...] += jnp.dot(rest, right(1 - k), preferred_element_type=F32)
+    cxs[...] += weighted(1 - k, (rest,))
     rcopy(cxs, cxr, ex_send.at[3], ex_recv.at[3], partner, m)
     pending.append(lambda: wait_bytes(cxr, ex_send.at[3]))
-    cond_ref[...] += jnp.dot(rest, right(k), preferred_element_type=F32)
+    cond_ref[...] += weighted(k, (rest,))
     wait_bytes(cxr, ex_recv.at[3])
     cond_ref[...] += cxr[...]
 
@@ -389,14 +406,14 @@
 def on_device(hidden_grads, weight_grad):
     dma = pltpu.SemaphoreType.DMA
     vm = pltpu.VMEM
-    return pl.pallas_call(
+    root, conditioned = pl.pallas_call(
         kernel,
-        out_shape=(jax.ShapeDtypeStruct((128, 64), F32), jax.ShapeDtypeStruct((128, 192), F32)),
-        in_specs=[pl.BlockSpec(memory_space=pl.ANY)] * 2,
+        out_shape=(jax.ShapeDtypeStruct((64, 128), F32), jax.ShapeDtypeStruct((192, 128), F32)),
+        in_specs=[pl.BlockSpec(memory_space=pltpu.HBM)] * 2,
         out_specs=(pl.BlockSpec(memory_space=pltpu.VMEM),) * 2,
         scratch_shapes=[
             vm((1024, 2048), BF16),
-            vm((128, 192), BF16),
+            vm((192, 128), BF16),
             vm((2, 32, 64, 128), BF16),
             vm((64, 64, 128), BF16),
             vm((8, 64, 128), F32), vm((8, 64, 128), F32),
@@ -408,17 +425,18 @@
             vm((64, 128), BF16), vm((64, 128), BF16),
             vm((16, 64, 128), BF16), vm((16, 64, 128), BF16),
             vm((128, 128), F32), vm((64, 128), F32),
-            vm((64, 128), F32), vm((64, 128), F32),
+            vm((64, 128), F32), vm((64, 128), F32), vm((128, 128), F32),
             vm((64, 128), BF16), vm((16, 64, 128), BF16),
-            vm((16, 128, 192), BF16),
-            vm((128, 192), F32), vm((128, 192), F32),
+            vm((16, 192, 128), BF16),
+            vm((192, 128), F32), vm((192, 128), F32),
             dma((2,)), dma, dma((3, CH)), dma, dma, dma((2,)), dma((2,)), dma,
             dma, dma, dma((2,)), dma((2,)), dma((3,)), dma((3,)), dma((2,)), dma((2,)), dma((4,)), dma((4,)),
-            dma((2,)), dma((2,)),
+            dma((2,)), dma((2,)), pltpu.SemaphoreType.REGULAR((4,)),
         ],
-        compiler_params=pltpu.CompilerParams(has_side_effects=True, collective_id=0, vmem_limit_bytes=48 * 1024 * 1024),
+        compiler_params=pltpu.CompilerParams(has_side_effects=True, collective_id=0, vmem_limit_bytes=66700000),
         name="kfac",
-    )(hidden_grads, weight_grad)
+    )(hidden_grads, weight_grad.T)
+    return root.T, conditioned.T
 
 
 def solution(mesh):

time: 94.6 us -> 87.4 us (0.924)
  Pallas kernels: 90.4 us -> 83.6 us
    pallas_call x1, Pallas kernels: 90.4 us -> 83.6 us  [on_device(): pl.pallas_call(kernel, out_shape=(jax.ShapeDtypeStruct((64, 128), F32), j...]
    pallas_call x2 -> x0, local copies, waits for them, and re-layouts: 1.44 us -> none  [on_device(): pl.pallas_call(kernel, out_shape=(jax.ShapeDtypeStruct((128, 64), F32), j...]
    unnamed x3 -> x2, local copies, waits for them, and re-layouts: 1.93 us -> 2.91 us
where the time goes in v3:
time: 87.4 us; the launch traced here: 87.2 us
  Pallas kernels  83.6 us (96%)
  local copies, waits for them, and re-layouts  2.91 us (3%)
    pallas_call x1, Pallas kernels, on_device(): pl.pallas_call(kernel, out_shape=(jax.ShapeDtypeStruct((64, 128), F32), j...  83.6 us
    unnamed x2, local copies, waits for them, and re-layouts  2.91 us

profile of v3, /device:TPU:1, one launch (start us, length us, event | category | flops | bytes accessed | tf_op | source)
XLA Modules:
  0.0 87.2 jit_solution(17711476364187789376)
XLA Ops:
  0.6 83.6 %kfac.1 = (f32[64,128]{1,0:T(8,128)}, f32[192,128]{1,0:T(8,128)}) custom-call(bf16[128,2048]{1,0:T(8,128)(2,1)} %x_hbm.1, bf16[192,128]{1,0:T(8,128)(2,1)} %bitcast.4), custom_call_target="tpu_custom_call" | custom-call | tf_op jit(solution)/shard_map/kfac/pallas_call | solution.py:409
  84.3 1.4 %copy.6 = f32[128,64]{0,1:T(8,128)} copy(f32[128,64]{0,1:T(8,128)} %bitcast.5) | data formatting | bytes 65536
  85.7 1.5 %copy.7 = f32[128,192]{0,1:T(8,128)} copy(f32[128,192]{0,1:T(8,128)} %bitcast.3) | data formatting | bytes 196608

commit v4 on v3

--- a/solution.py
+++ b/solution.py
@@ -22,6 +22,10 @@
         device_id=(g, m), device_id_type=MESH,
     )
     cp.start()
+
+
+def far_first(t):
+    return 4 + div(t + 1, 2) * (1 - 2 * rem(t, 2))
 
 
 def wait_bytes(ref, sem):
@@ -195,20 +199,21 @@
                     sb[0, zs[t] * 4 + yo] = tile[:64]
                     sb[1, yo * 8 + zs[t]] = tile[64:]
 
-        @pl.loop(1, 9)
-        def _(i):
+        @pl.loop(0, 8)
+        def _(t):
+            i = far_first(t)
             xx, yy, zz = diagonal(0, i)
             dg, dm = place(xx, yy, zz, 0)
             piece = sb.at[0, pl.ds(zz * 4, 4)]
             there = pl.ds(z * 8 + 4 * k, 4)
             ready = rem(zz, 2) == parity
-            mine = jnp.logical_and(ready, jnp.logical_and(on_low, i == 8))
+            mine = jnp.logical_and(ready, jnp.logical_and(on_low, i == 0))
 
             @pl.when(mine)
             def _():
                 ra[there] = piece[...]
 
-            @pl.when(jnp.logical_and(ready, jnp.logical_not(jnp.logical_and(on_low, i == 8))))
+            @pl.when(jnp.logical_and(ready, jnp.logical_not(jnp.logical_and(on_low, i == 0))))
             def _():
                 rcopy(piece, ra.at[there], rs_send.at[0], rs_recv, dg, dm)
 
@@ -259,20 +264,21 @@
     wait_bytes(ssa.at[pl.ds(0, 7)], sr_recv.at[0])
     ssy[...] = jnp.sum(ssa[...], axis=0)
 
-    @pl.loop(1, 9)
-    def _(i):
+    @pl.loop(0, 8)
+    def _(t):
+        i = far_first(t)
         to = rem(second_slot + i, 8)
         acc = ra[to].astype(F32)
         for j in range(1, 8):
             acc = acc + ra[j * 8 + to].astype(F32)
         dg, dm = place(*diagonal((1 - k) * i, k * i), k)
 
-        @pl.when(i == 8)
+        @pl.when(i == 0)
         def _():
             rb[second_slot] = acc
             ssb[second_slot] = ssy[...]
 
-        @pl.when(i < 8)
+        @pl.when(i > 0)
         def _():
             sb2[to] = acc
             rcopy(sb2.at[to], rb.at[second_slot], rs2_send, rs2_recv, dg, dm)
@@ -293,10 +299,12 @@
     col_slot = 2 * rem(m, 8) + k
     own_row, own_col = row_core == k, col_core == k
 
-    def along_row(src, dst, n):
+    def along_row(src, dst, n, ordered=False):
         @pl.loop(0, 16)
-        def _(i):
-            dg = 2 * rem(c + i, 16) + row_core
+        def _(t):
+            dx = 1 - rem(t, 2)
+            to = div(t, 2) if ordered else rem(z + far_first(div(t, 2)), 8)
+            dg = 2 * (2 * to + rem(xh + dx, 2)) + row_core
 
             @pl.when(dg == g)
             def _():
@@ -308,8 +316,9 @@
 
     def along_col(src, dst, n):
         @pl.loop(0, 16)
-        def _(i):
-            dg, dm = 2 * c + col_core, rem(m + i, 16)
+        def _(t):
+            dy, dx = far_first(div(t, 2)), 1 - rem(t, 2)
+            dg, dm = 2 * c + col_core, 2 * rem(y + dy, 8) + rem(xl + dx, 2)
             mine = jnp.logical_and(dg == g, dm == m)
 
             @pl.when(mine)
@@ -365,7 +374,7 @@
     unit = jnp.where(row_ids == col_ids, 2.25, 0.0).astype(F32)
     zz_tile = unit - 2.4375 * it + 1.6875 * sq + higher
     qb[...] = (higher - 2.4375 * (it - it16.astype(F32)) + 1.6875 * (sq - sq16.astype(F32))).astype(BF16)
-    along_row(qb, qp, 2)
+    along_row(qb, qp, 2, ordered=True)
     zb[...] = zz_tile
     rcopy(zb, zx, ex_send.at[2], ex_recv.at[2], partner, m)
     pending.append(lambda: wait_some(qp, row_send.at[2], own_row))
@@ -433,7 +442,7 @@
             dma, dma, dma((2,)), dma((2,)), dma((3,)), dma((3,)), dma((2,)), dma((2,)), dma((4,)), dma((4,)),
             dma((2,)), dma((2,)), pltpu.SemaphoreType.REGULAR((4,)),
         ],
-        compiler_params=pltpu.CompilerParams(has_side_effects=True, collective_id=0, vmem_limit_bytes=66700000),
+        compiler_params=pltpu.CompilerParams(has_side_effects=True, collective_id=0, vmem_limit_bytes=56000000),
         name="kfac",
     )(hidden_grads, weight_grad.T)
     return root.T, conditioned.T

time: 87.4 us -> 82.5 us (0.944)
  Pallas kernels: 83.6 us -> 79.3 us
    pallas_call x1, Pallas kernels: 83.6 us -> 79.3 us  [on_device(): pl.pallas_call(kernel, out_shape=(jax.ShapeDtypeStruct((64, 128), F32), j...]
    unnamed x2 -> x4, local copies, waits for them, and re-layouts: 2.91 us -> 2.05 us
where the time goes in v4:
time: 82.5 us; the launch traced here: 82 us
  Pallas kernels  79.3 us (96%)
  local copies, waits for them, and re-layouts  2.05 us (2%)
    pallas_call x1, Pallas kernels, on_device(): pl.pallas_call(kernel, out_shape=(jax.ShapeDtypeStruct((64, 128), F32), j...  79.3 us
    unnamed x4, local copies, waits for them, and re-layouts  2.05 us

profile of v4, /device:TPU:1, one launch (start us, length us, event | category | flops | bytes accessed | tf_op | source)
XLA Modules:
  0.0 82.0 jit_solution(1428134995246724665)
XLA Ops:
  0.6 0.0 copy-start
  0.6 0.8 copy-done
  1.4 79.3 %kfac.1 = (f32[64,128]{1,0:T(8,128)S(1)}, f32[192,128]{1,0:T(8,128)S(1)}) custom-call(bf16[128,2048]{1,0:T(8,128)(2,1)} %x_hbm.1, bf16[192,128]{1,0:T(8,128)(2,1)S(1)} %bitcast.4), custom_call_target="tpu_custom_call" | custom-call | tf_op jit(solution)/shard_map/kfac/pallas_call | solution.py:418
  80.8 0.6 copy.6
  81.4 0.6 copy.7
Async XLA Ops:
  0.6 0.8 copy-start

commit v5 on v3

--- a/solution.py
+++ b/solution.py
@@ -10,7 +10,7 @@
 MESH = pl.DeviceIdType.MESH
 F32 = jnp.float32
 BF16 = jnp.bfloat16
-CH = 4
+CH = 8
 ROWS = 128 // CH
 rem = lax.rem
 div = lax.div
@@ -22,6 +22,9 @@
         device_id=(g, m), device_id_type=MESH,
     )
     cp.start()
+
+
+FAR_FIRST = (4, 3, 5, 2, 6, 1, 7, 0)
 
 
 def wait_bytes(ref, sem):
@@ -69,10 +72,6 @@
     def greet(dg, dm):
         pl.semaphore_signal(barrier, inc=1, device_id=(dg, dm), device_id_type=MESH)
 
-    def diagonal(dy, dz):
-        yy, zz = rem(y + dy, 8), rem(z + dz, 8)
-        return rem(role + 24 - 2 * yy - zz, 4), yy, zz
-
     greet(partner, m)
     for step in (1, 7):
         greet(*place(rem(x + step, 4), y, z, k))
@@ -98,10 +97,8 @@
     def rows(slot, ch):
         return pl.ds(pl.multiple_of(slot * 128 + ch * ROWS, ROWS), ROWS)
 
-    def diagonal(dy, dz):
-        yy, zz = rem(y + dy, 8), rem(z + dz, 8)
-        return rem(role + 24 - 2 * yy - zz, 4), yy, zz
-
+    zs_at = [z] + [rem(z + i, 8) for i in range(1, 8)]
+    ys_at = [y] + [rem(y + i, 8) for i in range(1, 8)]
     pending = []
 
     load_x.wait()
@@ -125,17 +122,16 @@
     w_kept = w_core == k
 
     def spread_w():
-        @pl.loop(1, 9)
-        def _(i):
-            mine = jnp.logical_and(i == 8, w_kept)
-
-            @pl.when(mine)
-            def _():
-                wp[w_slot] = wv[...]
-
-            @pl.when(jnp.logical_not(mine))
-            def _():
-                rcopy(wv, wp.at[w_slot], w_send.at[0], w_recv.at[0], *place(x, rem(y + i, 8), z, w_core))
+        for i in range(1, 8):
+            rcopy(wv, wp.at[w_slot], w_send.at[0], w_recv.at[0], *place(x, ys_at[i], z, w_core))
+
+        @pl.when(w_kept)
+        def _():
+            wp[w_slot] = wv[...]
+
+        @pl.when(jnp.logical_not(w_kept))
+        def _():
+            rcopy(wv, wp.at[w_slot], w_send.at[0], w_recv.at[0], partner, m)
 
     def cross_w(n):
         some = wp.at[pl.ds(8 * xl + 4 * n, 4)]
@@ -176,10 +172,11 @@
     in_half = div(y, 4) == k
     on_low = k == 0
 
-    @pl.loop(0, 2)
-    def _(parity):
+    for odd in range(2):
+        parity = rem(z + odd, 2)
+
         @pl.loop(0, 2)
-        def _(turn):
+        def _(turn, parity=parity):
             q = parity + 2 * turn
             m0 = 8 * k + rem(role + 4 - q, 4)
             left = jnp.concatenate([cols(m0), cols(m0 + 4)], axis=1)
@@ -195,48 +192,49 @@
                     sb[0, zs[t] * 4 + yo] = tile[:64]
                     sb[1, yo * 8 + zs[t]] = tile[64:]
 
-        @pl.loop(1, 9)
-        def _(i):
-            xx, yy, zz = diagonal(0, i)
-            dg, dm = place(xx, yy, zz, 0)
+        for i in FAR_FIRST:
+            if i % 2 != odd:
+                continue
+            zz = zs_at[i]
             piece = sb.at[0, pl.ds(zz * 4, 4)]
             there = pl.ds(z * 8 + 4 * k, 4)
-            ready = rem(zz, 2) == parity
-            mine = jnp.logical_and(ready, jnp.logical_and(on_low, i == 8))
-
-            @pl.when(mine)
-            def _():
+            if i:
+                xx = rem(role + 24 - 2 * y - zz, 4)
+                rcopy(piece, ra.at[there], rs_send.at[0], rs_recv, *place(xx, y, zz, 0))
+                continue
+
+            @pl.when(on_low)
+            def _(piece=piece, there=there):
                 ra[there] = piece[...]
 
-            @pl.when(jnp.logical_and(ready, jnp.logical_not(jnp.logical_and(on_low, i == 8))))
-            def _():
-                rcopy(piece, ra.at[there], rs_send.at[0], rs_recv, dg, dm)
-
-    @pl.loop(1, 5)
-    def _(i):
+            @pl.when(jnp.logical_not(on_low))
+            def _(piece=piece, there=there):
+                rcopy(piece, ra.at[there], rs_send.at[0], rs_recv, partner, m)
+
+    for i in range(1, 5):
         yo = rem(y + i, 4)
         yy = 4 * k + yo
-        xx = rem(role + 24 - 2 * yy - z, 4)
-        dg, dm = place(xx, yy, z, 1)
+        dg, dm = place(rem(role + 24 - 2 * yy - z, 4), yy, z, 1)
         piece = sb.at[1, pl.ds(yo * 8, 8)]
         there = pl.ds(y * 8, 8)
         mine = jnp.logical_and(k == 1, yy == y)
 
         @pl.when(mine)
-        def _():
+        def _(piece=piece, there=there):
             ra[there] = piece[...]
 
         @pl.when(jnp.logical_not(mine))
-        def _():
+        def _(piece=piece, there=there, dg=dg, dm=dm):
             rcopy(piece, ra.at[there], rs_send.at[1], rs_recv, dg, dm)
 
     wait_bytes(sso, ss_sem.at[1])
     ssx[...] = ss[...] + sso[...]
     ssa[first_slot] = ssx[...]
 
-    @pl.loop(1, 8)
-    def _(i):
-        dg, dm = place(*diagonal(k * i, (1 - k) * i), k)
+    for i in FAR_FIRST[:7]:
+        yy = (1 - k) * y + k * ys_at[i]
+        zz = k * z + (1 - k) * zs_at[i]
+        dg, dm = place(rem(role + 24 - 2 * yy - zz, 4), yy, zz, k)
         rcopy(ssx, ssa.at[first_slot], sr_send.at[0], sr_recv.at[0], dg, dm)
 
     def wait_first(sem, sending):
@@ -259,24 +257,21 @@
     wait_bytes(ssa.at[pl.ds(0, 7)], sr_recv.at[0])
     ssy[...] = jnp.sum(ssa[...], axis=0)
 
-    @pl.loop(1, 9)
-    def _(i):
-        to = rem(second_slot + i, 8)
+    for i in FAR_FIRST:
+        yy = k * y + (1 - k) * ys_at[i]
+        zz = (1 - k) * z + k * zs_at[i]
+        to = (1 - k) * yy + k * zz
         acc = ra[to].astype(F32)
         for j in range(1, 8):
             acc = acc + ra[j * 8 + to].astype(F32)
-        dg, dm = place(*diagonal((1 - k) * i, k * i), k)
-
-        @pl.when(i == 8)
-        def _():
-            rb[second_slot] = acc
-            ssb[second_slot] = ssy[...]
-
-        @pl.when(i < 8)
-        def _():
+        if i:
+            dg, dm = place(rem(role + 24 - 2 * yy - zz, 4), yy, zz, k)
             sb2[to] = acc
             rcopy(sb2.at[to], rb.at[second_slot], rs2_send, rs2_recv, dg, dm)
             rcopy(ssy, ssb.at[second_slot], sr_send.at[1], sr_recv.at[1], dg, dm)
+        else:
+            rb[second_slot] = acc
+            ssb[second_slot] = ssy[...]
 
     pending.append(lambda: wait_bytes(rb.at[pl.ds(0, 7)], rs2_send))
     pending.append(lambda: wait_bytes(ssb.at[pl.ds(0, 7)], sr_send.at[1]))
@@ -293,32 +288,36 @@
     col_slot = 2 * rem(m, 8) + k
     own_row, own_col = row_core == k, col_core == k
 
+    def keep_or_send(mine, src, dst, send, recv, dg, dm):
+        @pl.when(mine)
+        def _():
+            dst[...] = src[...]
+
+        @pl.when(jnp.logical_not(mine))
+        def _():
+            rcopy(src, dst, send, recv, dg, dm)
+
+    def exchange(row_src, row_dst, col_src, col_dst, n):
+        row_to, col_to = row_dst.at[row_slot], col_dst.at[col_slot]
+        rs, rr, cs, cr = row_send.at[n], row_recv.at[n], col_send.at[n], col_recv.at[n]
+        for i in FAR_FIRST:
+            for across in (1, 0):
+                xx, ww = (1 - xh, 1 - xl) if across else (xh, xl)
+                rg, cg, cm = 4 * zs_at[i] + 2 * xx + row_core, 2 * c + col_core, 2 * ys_at[i] + ww
+                if i or across:
+                    rcopy(row_src, row_to, rs, rr, rg, m)
+                    rcopy(col_src, col_to, cs, cr, cg, cm)
+                else:
+                    keep_or_send(own_row, row_src, row_to, rs, rr, rg, m)
+                    keep_or_send(own_col, col_src, col_to, cs, cr, cg, cm)
+
     def along_row(src, dst, n):
-        @pl.loop(0, 16)
-        def _(i):
-            dg = 2 * rem(c + i, 16) + row_core
-
-            @pl.when(dg == g)
-            def _():
-                dst[row_slot] = src[...]
-
-            @pl.when(dg != g)
-            def _():
-                rcopy(src, dst.at[row_slot], row_send.at[n], row_recv.at[n], dg, m)
-
-    def along_col(src, dst, n):
-        @pl.loop(0, 16)
-        def _(i):
-            dg, dm = 2 * c + col_core, rem(m + i, 16)
-            mine = jnp.logical_and(dg == g, dm == m)
-
-            @pl.when(mine)
-            def _():
-                dst[col_slot] = src[...]
-
-            @pl.when(jnp.logical_not(mine))
-            def _():
-                rcopy(src, dst.at[col_slot], col_send.at[n], col_recv.at[n], dg, dm)
+        to = dst.at[row_slot]
+        for zt in range(8):
+            dg = 4 * zt + 2 * (1 - xh) + row_core
+            rcopy(src, to, row_send.at[n], row_recv.at[n], dg, m)
+            dg = 4 * zt + 2 * xh + row_core
+            keep_or_send(dg == g, src, to, row_send.at[n], row_recv.at[n], dg, m)
 
     def side_by_side(ref):
         return jnp.concatenate(
@@ -335,8 +334,7 @@
 
     it16 = it.astype(BF16)
     yb[...] = it16
-    along_row(yb, rowp, 0)
-    along_col(yb, colp, 0)
+    exchange(yb, rowp, yb, colp, 0)
     wait_some(wp.at[pl.ds(0, 8)], w_recv.at[0], w_kept)
     cross_w(0)
     pending.append(lambda: wait_some(rowp, row_send.at[0], own_row))
@@ -349,8 +347,7 @@
     sq16 = sq.astype(BF16)
     ab[...] = sq16
     bb[...] = (0.0625 * sq - 0.5625 * it).astype(BF16)
-    along_row(ab, rowp2, 1)
-    along_col(bb, colp2, 1)
+    exchange(ab, rowp2, bb, colp2, 1)
     cross_w(1)
     pending.append(lambda: wait_bytes(wp.at[pl.ds(0, 8)], w_send.at[1]))
     pending.append(lambda: wait_some(rowp2, row_send.at[1], own_row))
@@ -433,9 +430,9 @@
             dma, dma, dma((2,)), dma((2,)), dma((3,)), dma((3,)), dma((2,)), dma((2,)), dma((4,)), dma((4,)),
             dma((2,)), dma((2,)), pltpu.SemaphoreType.REGULAR((4,)),
         ],
-        compiler_params=pltpu.CompilerParams(has_side_effects=True, collective_id=0, vmem_limit_bytes=66700000),
+        compiler_params=pltpu.CompilerParams(has_side_effects=True, collective_id=0, vmem_limit_bytes=56000000),
         name="kfac",
-    )(hidden_grads, weight_grad.T)
+    )(hidden_grads, pltpu.with_memory_space_constraint(weight_grad.T, pltpu.HBM))
     return root.T, conditioned.T
 
 

time: 87.4 us -> 81.2 us (0.929)
  Pallas kernels: 83.6 us -> 79.2 us
  local copies, waits for them, and re-layouts: 2.91 us -> 1.26 us
    pallas_call x1, Pallas kernels: 83.6 us -> 79.2 us  [on_device(): pl.pallas_call(kernel, out_shape=(jax.ShapeDtypeStruct((64, 128), F32), j...]
    unnamed x2, local copies, waits for them, and re-layouts: 2.91 us -> 1.26 us
where the time goes in v5:
time: 81.2 us; the launch traced here: 81.1 us
  Pallas kernels  79.2 us (98%)
  local copies, waits for them, and re-layouts  1.26 us (2%)
    pallas_call x1, Pallas kernels, on_device(): pl.pallas_call(kernel, out_shape=(jax.ShapeDtypeStruct((64, 128), F32), j...  79.2 us

profile of v5, /device:TPU:1, one launch (start us, length us, event | category | flops | bytes accessed | tf_op | source)
XLA Modules:
  0.0 81.1 jit_solution(5440677873500846349)
XLA Ops:
  0.6 79.2 %kfac.1 = (f32[64,128]{1,0:T(8,128)S(1)}, f32[192,128]{1,0:T(8,128)S(1)}) custom-call(bf16[128,2048]{1,0:T(8,128)(2,1)} %x_hbm.1, bf16[192,128]{1,0:T(8,128)(2,1)} %bitcast.5), custom_call_target="tpu_custom_call" | custom-call | tf_op jit(solution)/shard_map/kfac/pallas_call | solution.py:406
  79.9 0.6 copy.6
  80.5 0.6 copy.7

commit v6 on v5

--- a/solution.py
+++ b/solution.py
@@ -172,6 +172,17 @@
     in_half = div(y, 4) == k
     on_low = k == 0
 
+    def share_squares():
+        wait_bytes(sso, ss_sem.at[1])
+        ssx[...] = ss[...] + sso[...]
+        ssa[first_slot] = ssx[...]
+
+        for i in FAR_FIRST[:7]:
+            yy = (1 - k) * y + k * ys_at[i]
+            zz = k * z + (1 - k) * zs_at[i]
+            dg, dm = place(rem(role + 24 - 2 * yy - zz, 4), yy, zz, k)
+            rcopy(ssx, ssa.at[first_slot], sr_send.at[0], sr_recv.at[0], dg, dm)
+
     for odd in range(2):
         parity = rem(z + odd, 2)
 
@@ -192,6 +203,8 @@
                     sb[0, zs[t] * 4 + yo] = tile[:64]
                     sb[1, yo * 8 + zs[t]] = tile[64:]
 
+        if odd == 0:
+            share_squares()
         for i in FAR_FIRST:
             if i % 2 != odd:
                 continue
@@ -227,15 +240,6 @@
         def _(piece=piece, there=there, dg=dg, dm=dm):
             rcopy(piece, ra.at[there], rs_send.at[1], rs_recv, dg, dm)
 
-    wait_bytes(sso, ss_sem.at[1])
-    ssx[...] = ss[...] + sso[...]
-    ssa[first_slot] = ssx[...]
-
-    for i in FAR_FIRST[:7]:
-        yy = (1 - k) * y + k * ys_at[i]
-        zz = k * z + (1 - k) * zs_at[i]
-        dg, dm = place(rem(role + 24 - 2 * yy - zz, 4), yy, zz, k)
-        rcopy(ssx, ssa.at[first_slot], sr_send.at[0], sr_recv.at[0], dg, dm)
 
     def wait_first(sem, sending):
         full = sb.at[0]

time: 81.2 us -> 80.1 us (0.986)
  Pallas kernels: 79.2 us -> 78 us
    pallas_call x1, Pallas kernels: 79.2 us -> 78 us  [on_device(): pl.pallas_call(kernel, out_shape=(jax.ShapeDtypeStruct((64, 128), F32), j...]
where the time goes in v6:
time: 80.1 us; the launch traced here: 79.9 us
  Pallas kernels  78 us (97%)
  local copies, waits for them, and re-layouts  1.26 us (2%)
    pallas_call x1, Pallas kernels, on_device(): pl.pallas_call(kernel, out_shape=(jax.ShapeDtypeStruct((64, 128), F32), j...  78 us

profile of v6, /device:TPU:1, one launch (start us, length us, event | category | flops | bytes accessed | tf_op | source)
XLA Modules:
  0.0 79.9 jit_solution(15567028338589886273)
XLA Ops:
  0.6 78.0 %kfac.1 = (f32[64,128]{1,0:T(8,128)S(1)}, f32[192,128]{1,0:T(8,128)S(1)}) custom-call(bf16[128,2048]{1,0:T(8,128)(2,1)} %x_hbm.1, bf16[192,128]{1,0:T(8,128)(2,1)} %bitcast.5), custom_call_target="tpu_custom_call" | custom-call | tf_op jit(solution)/shard_map/kfac/pallas_call | solution.py:410
  78.7 0.6 copy.6
  79.3 0.6 copy.7
